TPU v7x, 32 devices: a whole 2x2x4 slice. The times are simulated.
32 devices in a mesh: expert: 8 (over y, x, core), dp: 4 (over z).
Axes of the slice: x: 2, y: 2, z: 4, core: 2. Of those that a mesh axis runs over, the one named last changes fastest.
Arguments:
- tokens: bfloat16 [256, 4096], P(('expert', 'dp')), may hold values from -6 to 6
- expert_ids: int32 [256, 2], P(('expert', 'dp')), may hold values from 0 to 7, all different within a row; in each aligned block of 8 rows (0 to 7, 8 to 15, ...) at most 4 rows name the same one
- gate_q: int32 [256, 2], P(('expert', 'dp')), may hold values from 1 to 255
- capacity: int32 [8], replicated, may hold values from 2 to 4, as said below
- w_gate: bfloat16 [8, 4096, 14336], P('dp', None, 'expert'), may hold values from -0.09375 to 0.09375
- w_up: bfloat16 [8, 4096, 14336], P('dp', None, 'expert'), may hold values from -0.09375 to 0.09375
- w_down: bfloat16 [8, 14336, 4096], P('dp', 'expert'), may hold values from -0.046875 to 0.046875
Outputs:
- mixed: bfloat16 [256, 4096], P(('expert', 'dp'))
Inputs may be any that keep to these rules, and one draw needn't show every extreme that they name: `expert_ids`: each token names two different experts; among the tokens of one device no expert is named more than 4 times. `capacity`: at least half of the experts have exactly 4.
All inputs are finite; a program needn't handle non-finite values.
Results may differ from a plain program's by a relative error of at most 0.005.
Values may be sent and summed in bfloat16 or wider, within the bound.
No kernel may reach another device: no remote copies, remote signals or barrier semaphores. Data moves between devices by JAX's collectives and lax.ppermute only.
A program may use at most 192 MiB of HBM per device.

v0:
```python
import jax
import jax.numpy as jnp
from jax import lax
from jax.experimental import pallas as pl
from jax.experimental.pallas import tpu as pltpu
from jax.sharding import PartitionSpec as P


CAP = 4
LANES = 128
MIB = 1 << 20


VMEM = pl.BlockSpec(memory_space=pltpu.VMEM)
ANY = pl.BlockSpec(memory_space=pl.ANY)
HBM = pl.BlockSpec(memory_space=pltpu.HBM)
SMEM = pl.BlockSpec(memory_space=pltpu.SMEM)


def params(mib):
    return pltpu.CompilerParams(vmem_limit_bytes=int(mib * MIB))


def in_hbm(array):
    return pltpu.with_memory_space_constraint(array, pltpu.HBM)


def iota(shape, dim):
    return lax.broadcasted_iota(jnp.int32, shape, dim)


def pack(tokens, ids, levels, capacity, place):
    rows, width = tokens.shape
    experts = capacity.shape[0]

    def body(place_ref, ids_hbm, level_hbm, cap_hbm, tok_hbm, out_ref, info_ref, ids_ref, level_ref, cap_ref, sems):
        copies = [
            pltpu.make_async_copy(src, dst, sems.at[i])
            for i, (src, dst) in enumerate(
                (
                    (ids_hbm, ids_ref),
                    (level_hbm, level_ref),
                    (cap_hbm, cap_ref),
                    (tok_hbm, out_ref.at[:, pl.ds(0, width)]),
                )
            )
        ]
        for copy in copies:
            copy.start()
        for copy in copies:
            copy.wait()
        eye = iota((rows, rows), 0) == iota((rows, rows), 1)
        lower = (iota((rows, rows), 1) < iota((rows, rows), 0)).astype(jnp.float32)
        expert = iota((rows, experts), 1).astype(jnp.float32)
        limits = cap_ref[...].astype(jnp.float32)

        def column(ref, k):
            return jnp.sum(jnp.where(eye, ref[k : k + 1, :].astype(jnp.float32), 0.0), axis=1, keepdims=True)

        named = [column(ids_ref, k) for k in range(2)]
        hot = [(expert == col).astype(jnp.float32) for col in named]
        before = jnp.dot(lower, hot[0] + hot[1], preferred_element_type=jnp.float32)
        level = [column(level_ref, k) for k in range(2)]
        total = level[0] + level[1]
        lane = iota((rows, LANES), 1)
        slots = jnp.full((rows, LANES), -1.0, jnp.float32)
        info = slots
        for k in range(2):
            rank = jnp.sum(hot[k] * before, axis=1, keepdims=True)
            limit = jnp.sum(hot[k] * limits, axis=1, keepdims=True)
            slot = jnp.where(rank < limit, named[k] * CAP + rank, -1.0)
            slots = jnp.where(lane == k, slot, slots)
            info = jnp.where(lane == k, slot, jnp.where(lane == 2 + k, level[k] / total, info))
        for i in range(2):
            info = jnp.where(lane == 4 + i, place_ref[i].astype(jnp.float32), info)
        out_ref[:, width:] = slots.astype(jnp.bfloat16)
        info_ref[...] = info

    return pl.pallas_call(
        body,
        in_specs=[SMEM] + [HBM] * 4,
        out_specs=[VMEM] * 2,
        out_shape=[
            jax.ShapeDtypeStruct((rows, width + LANES), jnp.bfloat16),
            jax.ShapeDtypeStruct((rows, LANES), jnp.float32),
        ],
        scratch_shapes=[
            pltpu.VMEM(ids.shape, jnp.int32),
            pltpu.VMEM(levels.shape, jnp.int32),
            pltpu.VMEM((1, experts), jnp.int32),
            pltpu.SemaphoreType.DMA((4,)),
        ],
        compiler_params=params(0.5),
        name="pack",
    )(place, *map(in_hbm, (ids, levels, capacity.reshape(1, experts), tokens)))


def mix_back(info, pieces, local):
    rows = info.shape[0]
    width = pieces[0].shape[1]
    span = local * CAP

    def body(info_ref, *refs):
        *ins, out_ref = refs
        here = info_ref[:, 4:5].astype(jnp.int32)
        row = iota((rows, span), 1)
        weights = []
        for q in range(len(ins)):
            group = here ^ q
            weight = jnp.zeros((rows, span), jnp.float32)
            for k in range(2):
                slot = info_ref[:, k : k + 1].astype(jnp.int32) - group * span
                if q % 2:
                    slot = jnp.where((slot < 0) | (slot >= span), -1, slot ^ CAP)
                weight = weight + jnp.where(row == slot, info_ref[:, 2 + k : 3 + k], 0.0)
            weights.append(weight)
        weight = jnp.concatenate(weights, axis=1)
        terms = []
        for _ in range(3):
            terms.append(weight.astype(jnp.bfloat16).astype(jnp.float32))
            weight = weight - terms[-1]
        terms = jnp.concatenate(terms + [jnp.zeros_like(weight)], axis=0).astype(jnp.bfloat16)
        blocks = jnp.concatenate([ref[...] for ref in ins], axis=0)
        sums = jnp.dot(terms, blocks, preferred_element_type=jnp.float32)
        total = sums[:rows] + sums[rows : 2 * rows] + sums[2 * rows : 3 * rows]
        out_ref[...] = total.astype(jnp.bfloat16)

    return pl.pallas_call(
        body,
        in_specs=[VMEM] * (1 + len(pieces)),
        out_specs=VMEM,
        out_shape=jax.ShapeDtypeStruct((rows, width), jnp.bfloat16),
        compiler_params=params(8),
        name="mix_back",
    )(info, *pieces)


def fetch(weights, member, splits, after):
    depth = weights.shape[1]
    parts = 4
    step = depth // parts
    count = len(splits)

    def body(w_ref, after_ref, *refs):
        outs, done_ref, sems = refs[:count], refs[count], refs[count + 1]
        copies = []
        for j, (first, width) in enumerate(splits):
            for i in range(parts):
                part = pl.ds(i * step, step)
                copies.append(
                    pltpu.make_async_copy(
                        w_ref.at[member, part, pl.ds(first, width)], outs[j].at[part], sems.at[j * parts + i]
                    )
                )
        for copy in copies:
            copy.start()
        for copy in copies:
            copy.wait()
        done_ref[...] = jnp.zeros_like(done_ref)

    *blocks, done = pl.pallas_call(
        body,
        in_specs=[HBM, ANY],
        out_specs=[VMEM] * (count + 1),
        out_shape=[pltpu.VMEM((depth, width), jnp.bfloat16) for _, width in splits]
        + [jax.ShapeDtypeStruct((8, LANES), jnp.float32)],
        scratch_shapes=[pltpu.SemaphoreType.DMA((parts * count,))],
        compiler_params=params(0.25),
    )(in_hbm(weights), after)
    return blocks, done


def joined(pieces, after):
    rows, width = pieces[0].shape
    count = len(pieces)

    def body(*refs):
        out_ref = refs[-1]
        for i in range(count):
            out_ref[i * rows : (i + 1) * rows, :] = refs[i][...]

    return pl.pallas_call(
        body,
        in_specs=[VMEM] * count + [ANY],
        out_specs=VMEM,
        out_shape=jax.ShapeDtypeStruct((count * rows, width), pieces[0].dtype),
        compiler_params=params(1),
    )(*pieces, after)


def picked(info, first, second, after):
    rows = first.shape[0]

    def body(info_ref, first_ref, second_ref, after_ref, out_ref):
        even = jnp.broadcast_to(info_ref[0:1, 5:6], (rows, 1)) == 0.0

        out_ref[...] = jnp.where(even, first_ref[...], second_ref[...])

    return pl.pallas_call(
        body,
        in_specs=[VMEM, VMEM, VMEM, ANY],
        out_specs=VMEM,
        out_shape=jax.ShapeDtypeStruct(first.shape, first.dtype),
        compiler_params=params(1),
    )(info, first, second, after)


def experts_kernel(pieces, info, held, tile, w_gate, w_up, w_down):
    local, width, units = w_gate.shape
    groups = len(pieces)
    piece_rows = pieces[0].shape[0]
    tokens = groups * piece_rows
    slots = tokens // 8 * CAP
    steps = units // tile
    down_steps = width // tile
    ring = 6
    batch = 2
    half = groups // 2 * piece_rows
    order = [(matrix, member) for member in range(local) for matrix in range(2)]
    given = [block for key in order for block in held[key]]

    def body(*refs):
        piece_refs = refs[:groups]
        info_ref = refs[groups]
        given_refs = list(refs[groups + 1 : groups + 1 + len(given)])
        wg, wu, wd, mine, theirs, toks, rows, hid, buf, sems = refs[groups + 1 + len(given) :]

        tiles, stream = {}, []
        for key in order:
            at = 0
            for block in held[key]:
                ref = given_refs.pop(0)
                for n in range(block.shape[1] // tile):
                    tiles[key, at] = (ref, n)
                    at += 1
        for member in range(local):
            for n in range(steps):
                for matrix in range(2):
                    if ((matrix, member), n) not in tiles:
                        tiles[(matrix, member), n] = len(stream)
                        stream.append(((wg, wu)[matrix], member, n))

        downs = len(stream)
        jobs = downs + down_steps

        def copies(i):
            at = i % ring
            if i < downs:
                w, member, n = stream[i]
                pairs = [(w.at[member, :, pl.ds(n * tile, tile)], buf.at[at])]
            else:
                cols = pl.ds((i - downs) * tile, tile)
                pairs = [(wd.at[m, :, cols], buf.at[at, pl.ds(m * units, units)]) for m in range(local)]
            return [pltpu.make_async_copy(*pair, sems.at[at, j]) for j, pair in enumerate(pairs)]

        def start(i):
            if i < jobs:
                for copy in copies(i):
                    copy.start()

        def wait(i):
            for copy in copies(i):
                copy.wait()

        for i in range(ring):
            start(i)

        first = info_ref[0:1, 4:5].astype(jnp.int32) * (local * CAP)
        token_block = iota((tokens, slots), 0) // 8
        slot = iota((tokens, slots), 1)
        slot_block = slot // CAP
        slot_rank = slot % CAP
        pick = [jnp.zeros((tokens, slots), jnp.bool_) for _ in range(local)]
        for g in range(groups):
            toks[g * piece_rows : (g + 1) * piece_rows, :] = piece_refs[g][:, :width]
        for k in range(2):
            code = jnp.concatenate(
                [ref[:, width : width + LANES].astype(jnp.float32)[:, k : k + 1] for ref in piece_refs], axis=0
            ).astype(jnp.int32)
            for m in range(local):
                hit = (code - first == slot_rank + m * CAP) & (token_block == (slot_block ^ m))
                pick[m] = pick[m] | hit
        pickers = [p.astype(jnp.float32).T.astype(jnp.bfloat16) for p in pick]

        def place(n, carry):
            cols = pl.ds(pl.multiple_of(n * tile, tile), tile)
            for m in range(local):
                rows[m, :, cols] = jnp.dot(pickers[m], toks[:, cols], preferred_element_type=jnp.float32).astype(
                    jnp.bfloat16
                )
            return carry

        lax.fori_loop(0, width // tile, place, 0)

        def product(matrix, m, n):
            spot = tiles[(matrix, m), n]
            if isinstance(spot, tuple):
                ref, at = spot
                block = ref[:, at * tile : (at + 1) * tile]
            else:
                block = buf[spot % ring, :width, :]
            return jnp.dot(rows[m], block, preferred_element_type=jnp.float32)

        def streamed(m, n):
            return [spot for matrix in range(2) if not isinstance(spot := tiles[(matrix, m), n], tuple)]

        waiting, ready = [], []
        for m in range(local):
            for n in range(steps):
                spots = streamed(m, n)
                if not spots:
                    ready.append(([(m, n)], []))
                elif waiting and len(waiting[-1][1]) + len(spots) <= batch:
                    waiting[-1][0].append((m, n))
                    waiting[-1][1].extend(spots)
                else:
                    waiting.append(([(m, n)], spots))
        turns = []
        while waiting or ready:
            turns += [queue.pop(0) for queue in (waiting, ready) if queue]
        for group, spots in turns:
            for spot in spots:
                wait(spot)
            for m, n in group:
                gate = product(0, m, n)
                up = product(1, m, n)
                act = gate * (1.0 / (1.0 + jnp.exp(-gate))) * up
                hid[m, :, n * tile : (n + 1) * tile] = act.astype(jnp.bfloat16)
            for spot in spots:
                start(spot + ring)

        low = iota((8, tile), 0) < CAP
        for n in range(down_steps):
            cols = slice(n * tile, (n + 1) * tile)
            if n % batch == 0:
                for i in range(n, min(n + batch, down_steps)):
                    wait(downs + i)
            slot_at = (downs + n) % ring
            outs = [
                jnp.dot(hid[m], buf[slot_at, m * units : (m + 1) * units, :], preferred_element_type=jnp.float32)
                for m in range(local)
            ]
            start(downs + n + ring)
            for j in range(slots // 8):
                a, b = (out[j * 8 : (j + 1) * 8] for out in outs)
                pair = jnp.concatenate([jnp.where(low, a, b), jnp.where(low, b, a)], axis=0)
                at = j * 16
                if at < half:
                    mine[at : at + 16, cols] = pair
                else:
                    theirs[at - half : at - half + 16, cols] = pair.astype(jnp.bfloat16)

    bf16 = jnp.bfloat16
    return pl.pallas_call(
        body,
        in_specs=[VMEM] * (groups + 1 + len(given)) + [HBM] * 3,
        out_specs=[VMEM] * 2,
        out_shape=[
            jax.ShapeDtypeStruct((half, width), jnp.float32),
            jax.ShapeDtypeStruct((half, width), bf16),
        ],
        scratch_shapes=[
            pltpu.VMEM((tokens, width), bf16),
            pltpu.VMEM((local, slots, width), bf16),
            pltpu.VMEM((local, slots, units), bf16),
            pltpu.VMEM((ring, max(width, local * units), tile), bf16),
            pltpu.SemaphoreType.DMA((ring, local)),
        ],
        compiler_params=params(18.2),
        name="experts",
    )(*pieces, info, *given, *map(in_hbm, (w_gate, w_up, w_down)))


def flip(size, bits):
    return [(i, i ^ bits) for i in range(size)]


def fast(tokens, expert_ids, gate_q, capacity, w_gate, w_up, w_down):
    size = lax.axis_size("expert")
    depth = lax.axis_size("dp")
    local, _, units = w_gate.shape
    core = jnp.bitwise_and(lax.axis_index("expert"), 1)
    place = jnp.stack([lax.axis_index("dp"), core]).astype(jnp.int32)
    mixed = [(i, i ^ (2 if i % 2 == 0 else 4)) for i in range(size)]

    packed, info = pack(tokens, expert_ids.T, gate_q.T, capacity, place)
    along = [packed] + [lax.ppermute(packed, "dp", flip(depth, k)) for k in range(1, depth)]
    tile = 256
    some, rest = 2 * tile, units - 4 * tile
    whole = ((0, some), (some, some), (2 * some, rest))
    gate0, gate0_done = fetch(w_gate, 0, whole, packed)
    base = joined(along, gate0_done)
    side_a = lax.ppermute(base, "expert", flip(size, 2))
    side_b = lax.ppermute(base, "expert", flip(size, 4))
    other_base = lax.ppermute(base, "expert", flip(size, 1))
    up0, up0_done = fetch(w_up, 0, whole, base)
    relay = picked(info, side_b, side_a, up0_done)
    across = lax.ppermute(relay, "expert", mixed)
    other_a = lax.ppermute(side_a, "expert", flip(size, 1))
    other_b = lax.ppermute(side_b, "expert", flip(size, 1))
    gate1, _ = fetch(w_gate, 1, ((0, 1 * tile),), relay)
    other_across = lax.ppermute(across, "expert", flip(size, 1))
    pieces = [base, side_a, side_b, across, other_base, other_a, other_b, other_across]
    held = {(0, 0): gate0, (1, 0): up0, (0, 1): gate1, (1, 1): []}
    mine, theirs = experts_kernel(pieces, info, held, tile, w_gate, w_up, w_down)

    rows = mine.shape[0] // 4
    back = lax.ppermute(theirs, "expert", flip(size, 1))
    quarter = [
        mine[i * rows : (i + 1) * rows] + back[i * rows : (i + 1) * rows].astype(jnp.float32) for i in range(4)
    ]
    got = lax.ppermute(quarter[3].astype(jnp.bfloat16), "expert", mixed).astype(jnp.float32)
    to_a = (quarter[1] + jnp.where(core == 0, 0.0, got)).astype(jnp.bfloat16)
    to_b = (quarter[2] + jnp.where(core == 0, got, 0.0)).astype(jnp.bfloat16)
    from_a = lax.ppermute(to_a, "expert", flip(size, 2))
    from_b = lax.ppermute(to_b, "expert", flip(size, 4))
    total = (quarter[0] + from_a.astype(jnp.float32) + from_b.astype(jnp.float32)).astype(jnp.bfloat16)
    block = rows // depth
    parts = [total[k * block : (k + 1) * block] for k in range(depth)]
    home = [parts[0]] + [lax.ppermute(parts[k], "dp", flip(depth, k)) for k in range(1, depth)]
    return mix_back(info, home, local)


EXPERTS = 8
D = 4096


def slot_table(expert_ids, capacity):
    flat_ids = expert_ids.reshape(-1)
    matches = (flat_ids[:, None] == jnp.arange(EXPERTS, dtype=jnp.int32)[None, :]).astype(jnp.int32)
    before = jnp.cumsum(matches, axis=0) - matches
    rank_in = jnp.sum(before * matches, axis=1)
    limit_of = jnp.sum(matches * capacity[None, :], axis=1)
    slot_of = flat_ids * CAP + rank_in
    chosen = slot_of[None, :] == jnp.arange(EXPERTS * CAP, dtype=jnp.int32)[:, None]
    return chosen & (rank_in < limit_of)[None, :]


def general(tokens, expert_ids, gate_q, capacity, w_gate, w_up, w_down):
    local_experts = w_gate.shape[0]
    groups = lax.axis_size("dp")
    own_table = slot_table(expert_ids, capacity)
    levels = gate_q.astype(jnp.float32)
    mixes = (levels / jnp.sum(levels, axis=1, keepdims=True)).reshape(-1)
    picker = own_table.reshape(EXPERTS * CAP, -1, 2).sum(axis=2).astype(jnp.bfloat16)
    slot_rows = jnp.dot(picker, tokens, preferred_element_type=jnp.float32).astype(jnp.bfloat16)
    slot_rows = slot_rows.reshape(EXPERTS, CAP, D)
    arrived = lax.all_to_all(slot_rows, "dp", split_axis=0, concat_axis=0, tiled=True)
    shard_piece = lax.all_gather(arrived[None], "expert", axis=0, tiled=True)
    amount = shard_piece.shape[0]
    blocks = shard_piece.reshape(amount, groups, local_experts, CAP, D)
    pieces = []
    for member in range(local_experts):
        row_block = blocks[:, :, member].reshape(-1, D)
        gate_val = jnp.dot(row_block, w_gate[member], preferred_element_type=jnp.float32)
        up_value = jnp.dot(row_block, w_up[member], preferred_element_type=jnp.float32)
        result = (jax.nn.silu(gate_val) * up_value).astype(jnp.bfloat16)
        pieces.append(result.reshape(amount, groups, CAP, -1))
    hidden = jnp.stack(pieces, axis=2)
    flat_hidden = hidden.reshape(-1, hidden.shape[-1])
    rows_here = groups * local_experts * CAP
    picked = flat_hidden
    picked = picked.reshape(-1, local_experts, CAP, flat_hidden.shape[-1])
    products = []
    for member in range(local_experts):
        products.append(
            jnp.einsum(
                "mcf,fd->mcd", picked[:, member], w_down[member], preferred_element_type=jnp.float32
            )
        )
    summed = lax.psum_scatter(
        jnp.stack(products, axis=1).reshape(lax.axis_size("expert") * rows_here, -1),
        "expert",
        scatter_dimension=0,
        tiled=True,
    )
    returned = lax.all_to_all(summed, "dp", split_axis=0, concat_axis=0, tiled=True)
    combine = own_table.astype(jnp.float32) * mixes[None, :]
    spread = jnp.einsum("sa,sd->ad", combine, returned, precision=lax.Precision.HIGHEST)
    mixed = spread.reshape(-1, 2, spread.shape[-1]).sum(axis=1)
    return mixed.astype(jnp.bfloat16)


def per_device(tokens, expert_ids, gate_q, capacity, w_gate, w_up, w_down):
    suits = (
        w_gate.shape[0] == 2
        and lax.axis_size("expert") == 8
        and lax.axis_size("dp") == 4
        and tokens.shape[0] == 8
    )
    args = (tokens, expert_ids, gate_q, capacity, w_gate, w_up, w_down)
    if not suits:
        return general(*args)
    return fast(*args)


def solution(mesh):
    in_specs = (
        P(("expert", "dp"), None),
        P(("expert", "dp"), None),
        P(("expert", "dp"), None),
        P(),
        P("dp", None, "expert"),
        P("dp", None, "expert"),
        P("dp", "expert", None),
    )
    out_specs = P(("expert", "dp"), None)
    return jax.shard_map(
        per_device, mesh=mesh, in_specs=in_specs, out_specs=out_specs, check_vma=False
    )
```

profile of v0, /device:TPU:0, one launch (start us, length us, event | category | flops | bytes accessed | tf_op | source)
XLA Modules:
  0.0 80.7 jit_solution(10145375340798376457)
XLA Ops:
  0.0 0.1 pad_add_fusion.place_ref
  0.1 1.7 %pack.1 = (bf16[8,4224]{1,0:T(8,128)(2,1)S(1)}, f32[8,128]{1,0:T(8,128)S(1)}) custom-call(s32[2]{0:T(128)S(1)} %pad_add_fusion.place_ref, s32[2,8]{1,0:T(2,128)} %bitcast.5, s32[2,8]{1,0:T(2,128)} %bitcast.6, s32[1,8]{1,0:T(1,128)} %bitcast.7, bf16[8,4096]{1,0:T(8,128)(2,1)} %tok_hbm.1), custom_call_target="tpu_custom_call" | custom-call | tf_op jit(solution)/shard_map/pack/pallas_call | solution.py:79
  1.8 5.1 %collective-permute-start.2 = (bf16[8,4224]{1,0:T(8,128)(2,1)S(1)}, bf16[8,4224]{1,0:T(8,128)(2,1)S(1)}, u32[]{:S(2)}, u32[]{:S(2)}) collective-permute-start(bf16[8,4224]{1,0:T(8,128)(2,1)S(1)} %get-tuple-element.19.after_ref.refs_0_), channel_id=1, source_target_pairs={{0,3},{1,2},{2,1},{3,0},{4,7},{5,6},{6,5},{7,4},{8,11},{9,10},{10,... | collective-permute-start | bytes 202760 | tf_op jit(solution)/shard_map/ppermute | solution.py:387
  7.0 0.0 collective-permute-start.1
  7.0 0.6 collective-permute-start
  7.6 5.4 %shard_map.73 = (bf16[4096,512]{1,0:T(8,128)(2,1)S(1)}, bf16[4096,512]{1,0:T(8,128)(2,1)S(1)}, bf16[4096,768]{1,0:T(8,128)(2,1)S(1)}, f32[8,128]{1,0:T(8,128)S(1)}) custom-call(bf16[2,4096,1792]{2,1,0:T(8,128)(2,1)} %refs_16_.1, bf16[8,4224]{1,0:T(8,128)(2,1)S(1)} %get-tuple-element.19.after_ref.refs_0_), custom_call_target="tpu_custom_call" | custom-call | tf_op jit(solution)/shard_map/pallas_call | solution.py:161
  13.1 1.7 %collective-permute-start.4 = (bf16[32,4224]{1,0:T(8,128)(2,1)S(1)}, bf16[32,4224]{1,0:T(8,128)(2,1)S(1)}, u32[]{:S(2)}, u32[]{:S(2)}) collective-permute-start(bf16[32,4224]{1,0:T(8,128)(2,1)S(1)} %shard_map.74.after_ref.refs_0_), channel_id=1, source_target_pairs={{0,16},{4,20},{8,24},{12,28},{16,0},{20,4},{24,8},{28,12},{1,17},{... | collective-permute-start | bytes 811016 | tf_op jit(solution)/shard_map/ppermute | solution.py:394
  14.8 1.5 %collective-permute-start.3 = (bf16[32,4224]{1,0:T(8,128)(2,1)S(1)}, bf16[32,4224]{1,0:T(8,128)(2,1)S(1)}, u32[]{:S(2)}, u32[]{:S(2)}) collective-permute-start(bf16[32,4224]{1,0:T(8,128)(2,1)S(1)} %shard_map.74.after_ref.refs_0_), channel_id=1, source_target_pairs={{0,8},{4,12},{8,0},{12,4},{16,24},{20,28},{24,16},{28,20},{1,9},{5... | collective-permute-start | bytes 811016 | tf_op jit(solution)/shard_map/ppermute | solution.py:393
  16.3 5.4 %shard_map.75 = (bf16[4096,512]{1,0:T(8,128)(2,1)S(1)}, bf16[4096,512]{1,0:T(8,128)(2,1)S(1)}, bf16[4096,768]{1,0:T(8,128)(2,1)S(1)}, f32[8,128]{1,0:T(8,128)S(1)}) custom-call(bf16[2,4096,1792]{2,1,0:T(8,128)(2,1)} %refs_17_.1, bf16[32,4224]{1,0:T(8,128)(2,1)S(1)} %shard_map.74.after_ref.refs_0_), custom_call_target="tpu_custom_call" | custom-call | tf_op jit(solution)/shard_map/pallas_call | solution.py:161
  21.8 0.4 collective-permute-done.3.second_ref.refs_1_
  22.2 0.1 shard_map.76.after_ref
  22.3 1.6 %collective-permute-start.5 = (bf16[32,4224]{1,0:T(8,128)(2,1)S(1)}, bf16[32,4224]{1,0:T(8,128)(2,1)S(1)}, u32[]{:S(2)}, u32[]{:S(2)}) collective-permute-start(bf16[32,4224]{1,0:T(8,128)(2,1)S(1)} %shard_map.76.after_ref), channel_id=1, source_target_pairs={{0,8},{4,20},{8,0},{12,28},{16,24},{20,4},{24,16},{28,12},{1,9},{5... | collective-permute-start | bytes 811016 | tf_op jit(solution)/shard_map/ppermute | solution.py:398
  23.8 0.5 collective-permute-start.8
  24.4 4.5 %collective-permute-done.5.refs_3_ = bf16[32,4224]{1,0:T(8,128)(2,1)S(1)} collective-permute-done((bf16[32,4224]{1,0:T(8,128)(2,1)S(1)}, bf16[32,4224]{1,0:T(8,128)(2,1)S(1)}, u32[]{:S(2)}, u32[]{:S(2)}) %collective-permute-start.5) | collective-permute-done | bytes 270368 | tf_op jit(solution)/shard_map/ppermute | solution.py:398
  28.8 2.2 %shard_map.77 = (bf16[4096,256]{1,0:T(8,128)(2,1)S(1)}, f32[8,128]{1,0:T(8,128)}) custom-call(bf16[2,4096,1792]{2,1,0:T(8,128)(2,1)} %refs_16_.1, bf16[32,4224]{1,0:T(8,128)(2,1)S(1)} %shard_map.76.after_ref), custom_call_target="tpu_custom_call" | custom-call | tf_op jit(solution)/shard_map/pallas_call | solution.py:161
  31.0 20.5 %experts.1 = (f32[128,4096]{1,0:T(8,128)S(1)}, bf16[128,4096]{1,0:T(8,128)(2,1)S(1)}) custom-call(bf16[32,4224]{1,0:T(8,128)(2,1)S(1)} %shard_map.74.after_ref.refs_0_, bf16[32,4224]{1,0:T(8,128)(2,1)S(1)} %collective-permute-done.3.second_ref.refs_1_, bf16[32,4224]{1,0:T(8,128)(2,1)S(1)} %collective-permute-done.4.first_ref.refs_2_, ...), custom_call_target="tpu_custom_call" | custom-call | tf_op jit(solution)/shard_map/experts/pallas_call | solution.py:354
  51.5 0.6 collective-permute-start.10
  52.1 2.3 %collective-permute-done.10 = bf16[128,4096]{1,0:T(8,128)(2,1)S(1)} collective-permute-done((bf16[128,4096]{1,0:T(8,128)(2,1)S(1)}, bf16[128,4096]{1,0:T(8,128)(2,1)S(1)}, u32[]{:S(2)}, u32[]{:S(2)}) %collective-permute-start.10) | collective-permute-done | bytes 1048608 | tf_op jit(solution)/shard_map/ppermute | solution.py:408
  54.4 0.8 add_convert_fusion.1
  55.1 1.5 %collective-permute-start.11 = (bf16[32,4096]{1,0:T(8,128)(2,1)}, bf16[32,4096]{1,0:T(8,128)(2,1)S(1)}, u32[]{:S(2)}, u32[]{:S(2)}) collective-permute-start(bf16[32,4096]{1,0:T(8,128)(2,1)} %add_convert_fusion.1), channel_id=1, source_target_pairs={{0,8},{4,20},{8,0},{12,28},{16,24},{20,4},{24,16},{28,12},{1,9},{5... | collective-permute-start | bytes 786440 | tf_op jit(solution)/shard_map/ppermute | solution.py:412
  56.6 5.1 %collective-permute-done.11 = bf16[32,4096]{1,0:T(8,128)(2,1)S(1)} collective-permute-done((bf16[32,4096]{1,0:T(8,128)(2,1)}, bf16[32,4096]{1,0:T(8,128)(2,1)S(1)}, u32[]{:S(2)}, u32[]{:S(2)}) %collective-permute-start.11) | collective-permute-done | bytes 262176 | tf_op jit(solution)/shard_map/ppermute | solution.py:412
  61.7 0.2 fusion.1
  61.9 1.6 %collective-permute-start.12 = (bf16[32,4096]{1,0:T(8,128)(2,1)S(1)}, bf16[32,4096]{1,0:T(8,128)(2,1)S(1)}, u32[]{:S(2)}, u32[]{:S(2)}) collective-permute-start(bf16[32,4096]{1,0:T(8,128)(2,1)S(1)} %get-tuple-element.31), channel_id=1, source_target_pairs={{0,8},{4,12},{8,0},{12,4},{16,24},{20,28},{24,16},{28,20},{1,9},{5... | collective-permute-start | bytes 786440 | tf_op jit(solution)/shard_map/ppermute | solution.py:415
  63.5 0.5 collective-permute-start.13
  64.0 5.7 %collective-permute-done.12 = bf16[32,4096]{1,0:T(8,128)(2,1)S(1)} collective-permute-done((bf16[32,4096]{1,0:T(8,128)(2,1)S(1)}, bf16[32,4096]{1,0:T(8,128)(2,1)S(1)}, u32[]{:S(2)}, u32[]{:S(2)}) %collective-permute-start.12) | collective-permute-done | bytes 262176 | tf_op jit(solution)/shard_map/ppermute | solution.py:415
  69.7 1.2 %collective-permute-done.13 = bf16[32,4096]{1,0:T(8,128)(2,1)S(1)} collective-permute-done((bf16[32,4096]{1,0:T(8,128)(2,1)S(1)}, bf16[32,4096]{1,0:T(8,128)(2,1)S(1)}, u32[]{:S(2)}, u32[]{:S(2)}) %collective-permute-start.13) | collective-permute-done | bytes 262176 | tf_op jit(solution)/shard_map/ppermute | solution.py:416
  70.9 0.1 add_convert_fusion
  71.1 3.4 %collective-permute-start.16 = (bf16[8,4096]{1,0:T(8,128)(2,1)S(1)}, bf16[8,4096]{1,0:T(8,128)(2,1)S(1)}, u32[]{:S(2)}, u32[]{:S(2)}) collective-permute-start(bf16[8,4096]{1,0:T(8,128)(2,1)S(1)} %get-tuple-element.33), channel_id=1, source_target_pairs={{0,3},{1,2},{2,1},{3,0},{4,7},{5,6},{6,5},{7,4},{8,11},{9,10},{10,... | collective-permute-start | bytes 196616 | tf_op jit(solution)/shard_map/ppermute | solution.py:420
  74.5 1.0 %collective-permute-start.14 = (bf16[8,4096]{1,0:T(8,128)(2,1)S(1)}, bf16[8,4096]{1,0:T(8,128)(2,1)S(1)}, u32[]{:S(2)}, u32[]{:S(2)}) collective-permute-start(bf16[8,4096]{1,0:T(8,128)(2,1)S(1)} %get-tuple-element.35), channel_id=1, source_target_pairs={{0,1},{1,0},{2,3},{3,2},{4,5},{5,4},{6,7},{7,6},{8,9},{9,8},{10,11... | collective-permute-start | bytes 196616 | tf_op jit(solution)/shard_map/ppermute | solution.py:420
  75.5 1.8 %collective-permute-done.16.refs_3_ = bf16[8,4096]{1,0:T(8,128)(2,1)S(1)} collective-permute-done((bf16[8,4096]{1,0:T(8,128)(2,1)S(1)}, bf16[8,4096]{1,0:T(8,128)(2,1)S(1)}, u32[]{:S(2)}, u32[]{:S(2)}) %collective-permute-start.16) | collective-permute-done | bytes 65568 | tf_op jit(solution)/shard_map/ppermute | solution.py:420
  77.3 2.4 %collective-permute-done.15.refs_2_ = bf16[8,4096]{1,0:T(8,128)(2,1)S(1)} collective-permute-done((bf16[8,4096]{1,0:T(8,128)(2,1)S(1)}, bf16[8,4096]{1,0:T(8,128)(2,1)S(1)}, u32[]{:S(2)}, u32[]{:S(2)}) %collective-permute-start.15) | collective-permute-done | bytes 65568 | tf_op jit(solution)/shard_map/ppermute | solution.py:420
  79.7 1.1 %mix_back.1 = bf16[8,4096]{1,0:T(8,128)(2,1)} custom-call(f32[8,128]{1,0:T(8,128)S(1)} %get-tuple-element.18.info_ref.refs_8_, bf16[8,4096]{1,0:T(8,128)(2,1)S(1)} %get-tuple-element.36.refs_0_, bf16[8,4096]{1,0:T(8,128)(2,1)S(1)} %collective-permute-done.14.refs_1_, bf16[8,4096]{1,0:T(8,128)(2,1)S(1)} %collective-permute-done.15.refs_2_, ...), custom_call_target="tpu_custom_call" | custom-call | tf_op jit(solution)/shard_map/mix_back/pallas_call | solution.py:128
  (15 shorter events, 0.1 us)
Async XLA Ops:
  1.8 11.2 %collective-permute-start.2 = (bf16[8,4224]{1,0:T(8,128)(2,1)S(1)}, bf16[8,4224]{1,0:T(8,128)(2,1)S(1)}, u32[]{:S(2)}, u32[]{:S(2)}) collective-permute-start(bf16[8,4224]{1,0:T(8,128)(2,1)S(1)} %get-tuple-element.19.after_ref.refs_0_), channel_id=1, source_target_pairs={{0,3},{1,2},{2,1},{3,0},{4,7},{5,6},{6,5},{7,4},{8,11},{9,10},{10,... | collective-permute-start | bytes 202760 | tf_op jit(solution)/shard_map/ppermute | solution.py:387
  7.0 6.1 %collective-permute-start.1 = (bf16[8,4224]{1,0:T(8,128)(2,1)S(1)}, bf16[8,4224]{1,0:T(8,128)(2,1)S(1)}, u32[]{:S(2)}, u32[]{:S(2)}) collective-permute-start(bf16[8,4224]{1,0:T(8,128)(2,1)S(1)} %get-tuple-element.19.after_ref.refs_0_), channel_id=1, source_target_pairs={{0,2},{1,3},{2,0},{3,1},{4,6},{5,7},{6,4},{7,5},{8,10},{9,11},{10,... | collective-permute-start | bytes 202760 | tf_op jit(solution)/shard_map/ppermute | solution.py:387
  7.0 6.1 %collective-permute-start = (bf16[8,4224]{1,0:T(8,128)(2,1)S(1)}, bf16[8,4224]{1,0:T(8,128)(2,1)S(1)}, u32[]{:S(2)}, u32[]{:S(2)}) collective-permute-start(bf16[8,4224]{1,0:T(8,128)(2,1)S(1)} %get-tuple-element.19.after_ref.refs_0_), channel_id=1, source_target_pairs={{0,1},{1,0},{2,3},{3,2},{4,5},{5,4},{6,7},{7,6},{8,9},{9,8},{10,11... | collective-permute-start | bytes 202760 | tf_op jit(solution)/shard_map/ppermute | solution.py:387
  13.1 8.7 %collective-permute-start.4 = (bf16[32,4224]{1,0:T(8,128)(2,1)S(1)}, bf16[32,4224]{1,0:T(8,128)(2,1)S(1)}, u32[]{:S(2)}, u32[]{:S(2)}) collective-permute-start(bf16[32,4224]{1,0:T(8,128)(2,1)S(1)} %shard_map.74.after_ref.refs_0_), channel_id=1, source_target_pairs={{0,16},{4,20},{8,24},{12,28},{16,0},{20,4},{24,8},{28,12},{1,17},{... | collective-permute-start | bytes 811016 | tf_op jit(solution)/shard_map/ppermute | solution.py:394
  14.8 7.3 %collective-permute-start.3 = (bf16[32,4224]{1,0:T(8,128)(2,1)S(1)}, bf16[32,4224]{1,0:T(8,128)(2,1)S(1)}, u32[]{:S(2)}, u32[]{:S(2)}) collective-permute-start(bf16[32,4224]{1,0:T(8,128)(2,1)S(1)} %shard_map.74.after_ref.refs_0_), channel_id=1, source_target_pairs={{0,8},{4,12},{8,0},{12,4},{16,24},{20,28},{24,16},{28,20},{1,9},{5... | collective-permute-start | bytes 811016 | tf_op jit(solution)/shard_map/ppermute | solution.py:393
  22.3 6.5 %collective-permute-start.5 = (bf16[32,4224]{1,0:T(8,128)(2,1)S(1)}, bf16[32,4224]{1,0:T(8,128)(2,1)S(1)}, u32[]{:S(2)}, u32[]{:S(2)}) collective-permute-start(bf16[32,4224]{1,0:T(8,128)(2,1)S(1)} %shard_map.76.after_ref), channel_id=1, source_target_pairs={{0,8},{4,20},{8,0},{12,28},{16,24},{20,4},{24,16},{28,12},{1,9},{5... | collective-permute-start | bytes 811016 | tf_op jit(solution)/shard_map/ppermute | solution.py:398
  23.8 7.1 %collective-permute-start.6 = (bf16[32,4224]{1,0:T(8,128)(2,1)S(1)}, bf16[32,4224]{1,0:T(8,128)(2,1)S(1)}, u32[]{:S(2)}, u32[]{:S(2)}) collective-permute-start(bf16[32,4224]{1,0:T(8,128)(2,1)S(1)} %shard_map.74.after_ref.refs_0_), channel_id=1, source_target_pairs={{0,4},{4,0},{8,12},{12,8},{16,20},{20,16},{24,28},{28,24},{1,5},{5... | collective-permute-start | bytes 811016 | tf_op jit(solution)/shard_map/ppermute | solution.py:395
  23.8 7.2 %collective-permute-start.8 = (bf16[32,4224]{1,0:T(8,128)(2,1)S(1)}, bf16[32,4224]{1,0:T(8,128)(2,1)S(1)}, u32[]{:S(2)}, u32[]{:S(2)}) collective-permute-start(bf16[32,4224]{1,0:T(8,128)(2,1)S(1)} %collective-permute-done.4.first_ref.refs_2_), channel_id=1, source_target_pairs={{0,4},{4,0},{8,12},{12,8},{16,20},{20,16},{24,28},{28,24},{1,5},{5... | collective-permute-start | bytes 811016 | tf_op jit(solution)/shard_map/ppermute | solution.py:400
  24.3 6.7 %collective-permute-start.7 = (bf16[32,4224]{1,0:T(8,128)(2,1)S(1)}, bf16[32,4224]{1,0:T(8,128)(2,1)S(1)}, u32[]{:S(2)}, u32[]{:S(2)}) collective-permute-start(bf16[32,4224]{1,0:T(8,128)(2,1)S(1)} %collective-permute-done.3.second_ref.refs_1_), channel_id=1, source_target_pairs={{0,4},{4,0},{8,12},{12,8},{16,20},{20,16},{24,28},{28,24},{1,5},{5... | collective-permute-start | bytes 811016 | tf_op jit(solution)/shard_map/ppermute | solution.py:399
  28.8 2.2 %collective-permute-start.9 = (bf16[32,4224]{1,0:T(8,128)(2,1)S(1)}, bf16[32,4224]{1,0:T(8,128)(2,1)S(1)}, u32[]{:S(2)}, u32[]{:S(2)}) collective-permute-start(bf16[32,4224]{1,0:T(8,128)(2,1)S(1)} %collective-permute-done.5.refs_3_), channel_id=1, source_target_pairs={{0,4},{4,0},{8,12},{12,8},{16,20},{20,16},{24,28},{28,24},{1,5},{5... | collective-permute-start | bytes 811016 | tf_op jit(solution)/shard_map/ppermute | solution.py:402
  51.5 2.9 %collective-permute-start.10 = (bf16[128,4096]{1,0:T(8,128)(2,1)S(1)}, bf16[128,4096]{1,0:T(8,128)(2,1)S(1)}, u32[]{:S(2)}, u32[]{:S(2)}) collective-permute-start(bf16[128,4096]{1,0:T(8,128)(2,1)S(1)} %get-tuple-element.30), channel_id=1, source_target_pairs={{0,4},{4,0},{8,12},{12,8},{16,20},{20,16},{24,28},{28,24},{1,5},{5... | collective-permute-start | bytes 3145736 | tf_op jit(solution)/shard_map/ppermute | solution.py:408
  55.1 6.6 %collective-permute-start.11 = (bf16[32,4096]{1,0:T(8,128)(2,1)}, bf16[32,4096]{1,0:T(8,128)(2,1)S(1)}, u32[]{:S(2)}, u32[]{:S(2)}) collective-permute-start(bf16[32,4096]{1,0:T(8,128)(2,1)} %add_convert_fusion.1), channel_id=1, source_target_pairs={{0,8},{4,20},{8,0},{12,28},{16,24},{20,4},{24,16},{28,12},{1,9},{5... | collective-permute-start | bytes 786440 | tf_op jit(solution)/shard_map/ppermute | solution.py:412
  61.9 7.8 %collective-permute-start.12 = (bf16[32,4096]{1,0:T(8,128)(2,1)S(1)}, bf16[32,4096]{1,0:T(8,128)(2,1)S(1)}, u32[]{:S(2)}, u32[]{:S(2)}) collective-permute-start(bf16[32,4096]{1,0:T(8,128)(2,1)S(1)} %get-tuple-element.31), channel_id=1, source_target_pairs={{0,8},{4,12},{8,0},{12,4},{16,24},{20,28},{24,16},{28,20},{1,9},{5... | collective-permute-start | bytes 786440 | tf_op jit(solution)/shard_map/ppermute | solution.py:415
  63.5 7.5 %collective-permute-start.13 = (bf16[32,4096]{1,0:T(8,128)(2,1)S(1)}, bf16[32,4096]{1,0:T(8,128)(2,1)S(1)}, u32[]{:S(2)}, u32[]{:S(2)}) collective-permute-start(bf16[32,4096]{1,0:T(8,128)(2,1)S(1)} %get-tuple-element.32), channel_id=1, source_target_pairs={{0,16},{4,20},{8,24},{12,28},{16,0},{20,4},{24,8},{28,12},{1,17},{... | collective-permute-start | bytes 786440 | tf_op jit(solution)/shard_map/ppermute | solution.py:416
  71.1 6.2 %collective-permute-start.16 = (bf16[8,4096]{1,0:T(8,128)(2,1)S(1)}, bf16[8,4096]{1,0:T(8,128)(2,1)S(1)}, u32[]{:S(2)}, u32[]{:S(2)}) collective-permute-start(bf16[8,4096]{1,0:T(8,128)(2,1)S(1)} %get-tuple-element.33), channel_id=1, source_target_pairs={{0,3},{1,2},{2,1},{3,0},{4,7},{5,6},{6,5},{7,4},{8,11},{9,10},{10,... | collective-permute-start | bytes 196616 | tf_op jit(solution)/shard_map/ppermute | solution.py:420
  74.5 5.2 %collective-permute-start.15 = (bf16[8,4096]{1,0:T(8,128)(2,1)S(1)}, bf16[8,4096]{1,0:T(8,128)(2,1)S(1)}, u32[]{:S(2)}, u32[]{:S(2)}) collective-permute-start(bf16[8,4096]{1,0:T(8,128)(2,1)S(1)} %get-tuple-element.34), channel_id=1, source_target_pairs={{0,2},{1,3},{2,0},{3,1},{4,6},{5,7},{6,4},{7,5},{8,10},{9,11},{10,... | collective-permute-start | bytes 196616 | tf_op jit(solution)/shard_map/ppermute | solution.py:420
  74.5 5.2 %collective-permute-start.14 = (bf16[8,4096]{1,0:T(8,128)(2,1)S(1)}, bf16[8,4096]{1,0:T(8,128)(2,1)S(1)}, u32[]{:S(2)}, u32[]{:S(2)}) collective-permute-start(bf16[8,4096]{1,0:T(8,128)(2,1)S(1)} %get-tuple-element.35), channel_id=1, source_target_pairs={{0,1},{1,0},{2,3},{3,2},{4,5},{5,4},{6,7},{7,6},{8,9},{9,8},{10,11... | collective-permute-start | bytes 196616 | tf_op jit(solution)/shard_map/ppermute | solution.py:420
where the time goes:
time: 80.9 us; the launch traced here: 80.7 us
  Pallas kernels  36.4 us (45%)
  waiting for transfers between devices  23.3 us (29%)
  starting transfers between devices  19.7 us (24%)
  other arithmetic  1.16 us (1%)
    pallas_call x1, Pallas kernels, experts_kernel(): pl.pallas_call(body, in_specs=[VMEM] * (groups + 1 + len(given)) + [HBM]...  20.5 us
    pallas_call x3, Pallas kernels, fetch(): pl.pallas_call(body, in_specs=[HBM, ANY], out_specs=[VMEM] * (count + 1),...  13 us
    ppermute x3, starting transfers between devices, fast(): lax.ppermute(packed, 'dp', flip(depth, k))  5.78 us
    ppermute x1, waiting for transfers between devices, fast(): from_a = lax.ppermute(to_a, 'expert', flip(size, 2))  5.73 us
    ppermute x1, waiting for transfers between devices, fast(): lax.ppermute(quarter[3].astype(jnp.bfloat16), 'expert', mixed)  5.08 us
    ppermute x1, waiting for transfers between devices, fast(): across = lax.ppermute(relay, 'expert', mixed)  4.45 us
    ppermute x3, starting transfers between devices, fast(): lax.ppermute(parts[k], 'dp', flip(depth, k))  4.45 us
    ppermute x3, waiting for transfers between devices, fast(): lax.ppermute(parts[k], 'dp', flip(depth, k))  4.14 us
  transfers between devices with their start and end apart: 17, of which 8 were waited for; matrix products, arithmetic and copies ran while one was open for 0% of the time, Pallas kernels for 16%

commit v1 on v0

--- a/solution.py
+++ b/solution.py
@@ -213,7 +213,7 @@
     slots = tokens // 8 * CAP
     steps = units // tile
     down_steps = width // tile
-    ring = 6
+    ring = 5
     batch = 2
     half = groups // 2 * piece_rows
     order = [(matrix, member) for member in range(local) for matrix in range(2)]
@@ -366,7 +366,7 @@
             pltpu.VMEM((ring, max(width, local * units), tile), bf16),
             pltpu.SemaphoreType.DMA((ring, local)),
         ],
-        compiler_params=params(18.2),
+        compiler_params=params(16.2),
         name="experts",
     )(*pieces, info, *given, *map(in_hbm, (w_gate, w_up, w_down)))
 
@@ -398,7 +398,7 @@
     across = lax.ppermute(relay, "expert", mixed)
     other_a = lax.ppermute(side_a, "expert", flip(size, 1))
     other_b = lax.ppermute(side_b, "expert", flip(size, 1))
-    gate1, _ = fetch(w_gate, 1, ((0, 1 * tile),), relay)
+    gate1, _ = fetch(w_gate, 1, ((0, 2 * tile),), relay)
     other_across = lax.ppermute(across, "expert", flip(size, 1))
     pieces = [base, side_a, side_b, across, other_base, other_a, other_b, other_across]
     held = {(0, 0): gate0, (1, 0): up0, (0, 1): gate1, (1, 1): []}

time: 80.9 us -> 81.8 us (1.011)
  Pallas kernels: 36.4 us -> 37.3 us
  transfers between devices with their start and end apart: 17 -> 17, of which waited for: 8 -> 8; matrix products, arithmetic and copies ran while one was open for 0% -> 0% of each run, Pallas kernels for 16% -> 17%
where the time goes in v1:
time: 81.8 us; the launch traced here: 81.6 us
  Pallas kernels  37.3 us (46%)
  waiting for transfers between devices  23.3 us (28%)
  starting transfers between devices  19.7 us (24%)
  other arithmetic  1.16 us (1%)
    pallas_call x1, Pallas kernels, experts_kernel(): pl.pallas_call(body, in_specs=[VMEM] * (groups + 1 + len(given)) + [HBM]...  20.7 us
    pallas_call x3, Pallas kernels, fetch(): pl.pallas_call(body, in_specs=[HBM, ANY], out_specs=[VMEM] * (count + 1),...  13.7 us
    ppermute x3, starting transfers between devices, fast(): lax.ppermute(packed, 'dp', flip(depth, k))  5.78 us
    ppermute x1, waiting for transfers between devices, fast(): from_a = lax.ppermute(to_a, 'expert', flip(size, 2))  5.72 us
    ppermute x1, waiting for transfers between devices, fast(): lax.ppermute(quarter[3].astype(jnp.bfloat16), 'expert', mixed)  5.08 us
    ppermute x1, waiting for transfers between devices, fast(): across = lax.ppermute(relay, 'expert', mixed)  4.45 us
    ppermute x3, starting transfers between devices, fast(): lax.ppermute(parts[k], 'dp', flip(depth, k))  4.45 us
    ppermute x3, waiting for transfers between devices, fast(): lax.ppermute(parts[k], 'dp', flip(depth, k))  4.14 us
  transfers between devices with their start and end apart: 17, of which 8 were waited for; matrix products, arithmetic and copies ran while one was open for 0% of the time, Pallas kernels for 17%

profile of v1, /device:TPU:0, one launch (start us, length us, event | category | flops | bytes accessed | tf_op | source)
XLA Modules:
  0.0 81.6 jit_solution(15697753654657808679)
XLA Ops:
  0.0 0.1 pad_add_fusion.place_ref
  0.1 1.7 %pack.1 = (bf16[8,4224]{1,0:T(8,128)(2,1)S(1)}, f32[8,128]{1,0:T(8,128)S(1)}) custom-call(s32[2]{0:T(128)S(1)} %pad_add_fusion.place_ref, s32[2,8]{1,0:T(2,128)} %bitcast.5, s32[2,8]{1,0:T(2,128)} %bitcast.6, s32[1,8]{1,0:T(1,128)} %bitcast.7, bf16[8,4096]{1,0:T(8,128)(2,1)} %tok_hbm.1), custom_call_target="tpu_custom_call" | custom-call | tf_op jit(solution)/shard_map/pack/pallas_call | solution.py:79
  1.8 5.1 %collective-permute-start.2 = (bf16[8,4224]{1,0:T(8,128)(2,1)S(1)}, bf16[8,4224]{1,0:T(8,128)(2,1)S(1)}, u32[]{:S(2)}, u32[]{:S(2)}) collective-permute-start(bf16[8,4224]{1,0:T(8,128)(2,1)S(1)} %get-tuple-element.19.after_ref.refs_0_), channel_id=1, source_target_pairs={{0,3},{1,2},{2,1},{3,0},{4,7},{5,6},{6,5},{7,4},{8,11},{9,10},{10,... | collective-permute-start | bytes 202760 | tf_op jit(solution)/shard_map/ppermute | solution.py:387
  7.0 0.0 collective-permute-start.1
  7.0 0.6 collective-permute-start
  7.6 5.4 %shard_map.73 = (bf16[4096,512]{1,0:T(8,128)(2,1)S(1)}, bf16[4096,512]{1,0:T(8,128)(2,1)S(1)}, bf16[4096,768]{1,0:T(8,128)(2,1)S(1)}, f32[8,128]{1,0:T(8,128)S(1)}) custom-call(bf16[2,4096,1792]{2,1,0:T(8,128)(2,1)} %refs_16_.1, bf16[8,4224]{1,0:T(8,128)(2,1)S(1)} %get-tuple-element.19.after_ref.refs_0_), custom_call_target="tpu_custom_call" | custom-call | tf_op jit(solution)/shard_map/pallas_call | solution.py:161
  13.1 1.7 %collective-permute-start.4 = (bf16[32,4224]{1,0:T(8,128)(2,1)S(1)}, bf16[32,4224]{1,0:T(8,128)(2,1)S(1)}, u32[]{:S(2)}, u32[]{:S(2)}) collective-permute-start(bf16[32,4224]{1,0:T(8,128)(2,1)S(1)} %shard_map.74.after_ref.refs_0_), channel_id=1, source_target_pairs={{0,16},{4,20},{8,24},{12,28},{16,0},{20,4},{24,8},{28,12},{1,17},{... | collective-permute-start | bytes 811016 | tf_op jit(solution)/shard_map/ppermute | solution.py:394
  14.8 1.5 %collective-permute-start.3 = (bf16[32,4224]{1,0:T(8,128)(2,1)S(1)}, bf16[32,4224]{1,0:T(8,128)(2,1)S(1)}, u32[]{:S(2)}, u32[]{:S(2)}) collective-permute-start(bf16[32,4224]{1,0:T(8,128)(2,1)S(1)} %shard_map.74.after_ref.refs_0_), channel_id=1, source_target_pairs={{0,8},{4,12},{8,0},{12,4},{16,24},{20,28},{24,16},{28,20},{1,9},{5... | collective-permute-start | bytes 811016 | tf_op jit(solution)/shard_map/ppermute | solution.py:393
  16.3 5.4 %shard_map.75 = (bf16[4096,512]{1,0:T(8,128)(2,1)S(1)}, bf16[4096,512]{1,0:T(8,128)(2,1)S(1)}, bf16[4096,768]{1,0:T(8,128)(2,1)S(1)}, f32[8,128]{1,0:T(8,128)S(1)}) custom-call(bf16[2,4096,1792]{2,1,0:T(8,128)(2,1)} %refs_17_.1, bf16[32,4224]{1,0:T(8,128)(2,1)S(1)} %shard_map.74.after_ref.refs_0_), custom_call_target="tpu_custom_call" | custom-call | tf_op jit(solution)/shard_map/pallas_call | solution.py:161
  21.8 0.4 collective-permute-done.3.second_ref.refs_1_
  22.2 0.1 shard_map.76.after_ref
  22.3 1.6 %collective-permute-start.5 = (bf16[32,4224]{1,0:T(8,128)(2,1)S(1)}, bf16[32,4224]{1,0:T(8,128)(2,1)S(1)}, u32[]{:S(2)}, u32[]{:S(2)}) collective-permute-start(bf16[32,4224]{1,0:T(8,128)(2,1)S(1)} %shard_map.76.after_ref), channel_id=1, source_target_pairs={{0,8},{4,20},{8,0},{12,28},{16,24},{20,4},{24,16},{28,12},{1,9},{5... | collective-permute-start | bytes 811016 | tf_op jit(solution)/shard_map/ppermute | solution.py:398
  23.8 0.5 collective-permute-start.8
  24.4 4.5 %collective-permute-done.5.refs_3_ = bf16[32,4224]{1,0:T(8,128)(2,1)S(1)} collective-permute-done((bf16[32,4224]{1,0:T(8,128)(2,1)S(1)}, bf16[32,4224]{1,0:T(8,128)(2,1)S(1)}, u32[]{:S(2)}, u32[]{:S(2)}) %collective-permute-start.5) | collective-permute-done | bytes 270368 | tf_op jit(solution)/shard_map/ppermute | solution.py:398
  28.8 2.8 %shard_map.77 = (bf16[4096,512]{1,0:T(8,128)(2,1)S(1)}, f32[8,128]{1,0:T(8,128)}) custom-call(bf16[2,4096,1792]{2,1,0:T(8,128)(2,1)} %refs_16_.1, bf16[32,4224]{1,0:T(8,128)(2,1)S(1)} %shard_map.76.after_ref), custom_call_target="tpu_custom_call" | custom-call | tf_op jit(solution)/shard_map/pallas_call | solution.py:161
  31.7 20.7 %experts.1 = (f32[128,4096]{1,0:T(8,128)S(1)}, bf16[128,4096]{1,0:T(8,128)(2,1)S(1)}) custom-call(bf16[32,4224]{1,0:T(8,128)(2,1)S(1)} %shard_map.74.after_ref.refs_0_, bf16[32,4224]{1,0:T(8,128)(2,1)S(1)} %collective-permute-done.3.second_ref.refs_1_, bf16[32,4224]{1,0:T(8,128)(2,1)S(1)} %collective-permute-done.4.first_ref.refs_2_, ...), custom_call_target="tpu_custom_call" | custom-call | tf_op jit(solution)/shard_map/experts/pallas_call | solution.py:354
  52.4 0.6 collective-permute-start.10
  53.0 2.3 %collective-permute-done.10 = bf16[128,4096]{1,0:T(8,128)(2,1)S(1)} collective-permute-done((bf16[128,4096]{1,0:T(8,128)(2,1)S(1)}, bf16[128,4096]{1,0:T(8,128)(2,1)S(1)}, u32[]{:S(2)}, u32[]{:S(2)}) %collective-permute-start.10) | collective-permute-done | bytes 1048608 | tf_op jit(solution)/shard_map/ppermute | solution.py:408
  55.3 0.8 add_convert_fusion.1
  56.0 1.5 %collective-permute-start.11 = (bf16[32,4096]{1,0:T(8,128)(2,1)}, bf16[32,4096]{1,0:T(8,128)(2,1)S(1)}, u32[]{:S(2)}, u32[]{:S(2)}) collective-permute-start(bf16[32,4096]{1,0:T(8,128)(2,1)} %add_convert_fusion.1), channel_id=1, source_target_pairs={{0,8},{4,20},{8,0},{12,28},{16,24},{20,4},{24,16},{28,12},{1,9},{5... | collective-permute-start | bytes 786440 | tf_op jit(solution)/shard_map/ppermute | solution.py:412
  57.5 5.1 %collective-permute-done.11 = bf16[32,4096]{1,0:T(8,128)(2,1)S(1)} collective-permute-done((bf16[32,4096]{1,0:T(8,128)(2,1)}, bf16[32,4096]{1,0:T(8,128)(2,1)S(1)}, u32[]{:S(2)}, u32[]{:S(2)}) %collective-permute-start.11) | collective-permute-done | bytes 262176 | tf_op jit(solution)/shard_map/ppermute | solution.py:412
  62.6 0.2 fusion.1
  62.8 1.6 %collective-permute-start.12 = (bf16[32,4096]{1,0:T(8,128)(2,1)S(1)}, bf16[32,4096]{1,0:T(8,128)(2,1)S(1)}, u32[]{:S(2)}, u32[]{:S(2)}) collective-permute-start(bf16[32,4096]{1,0:T(8,128)(2,1)S(1)} %get-tuple-element.31), channel_id=1, source_target_pairs={{0,8},{4,12},{8,0},{12,4},{16,24},{20,28},{24,16},{28,20},{1,9},{5... | collective-permute-start | bytes 786440 | tf_op jit(solution)/shard_map/ppermute | solution.py:415
  64.4 0.5 collective-permute-start.13
  64.9 5.7 %collective-permute-done.12 = bf16[32,4096]{1,0:T(8,128)(2,1)S(1)} collective-permute-done((bf16[32,4096]{1,0:T(8,128)(2,1)S(1)}, bf16[32,4096]{1,0:T(8,128)(2,1)S(1)}, u32[]{:S(2)}, u32[]{:S(2)}) %collective-permute-start.12) | collective-permute-done | bytes 262176 | tf_op jit(solution)/shard_map/ppermute | solution.py:415
  70.6 1.2 %collective-permute-done.13 = bf16[32,4096]{1,0:T(8,128)(2,1)S(1)} collective-permute-done((bf16[32,4096]{1,0:T(8,128)(2,1)S(1)}, bf16[32,4096]{1,0:T(8,128)(2,1)S(1)}, u32[]{:S(2)}, u32[]{:S(2)}) %collective-permute-start.13) | collective-permute-done | bytes 262176 | tf_op jit(solution)/shard_map/ppermute | solution.py:416
  71.8 0.1 add_convert_fusion
  72.0 3.4 %collective-permute-start.16 = (bf16[8,4096]{1,0:T(8,128)(2,1)S(1)}, bf16[8,4096]{1,0:T(8,128)(2,1)S(1)}, u32[]{:S(2)}, u32[]{:S(2)}) collective-permute-start(bf16[8,4096]{1,0:T(8,128)(2,1)S(1)} %get-tuple-element.33), channel_id=1, source_target_pairs={{0,3},{1,2},{2,1},{3,0},{4,7},{5,6},{6,5},{7,4},{8,11},{9,10},{10,... | collective-permute-start | bytes 196616 | tf_op jit(solution)/shard_map/ppermute | solution.py:420
  75.4 1.0 %collective-permute-start.14 = (bf16[8,4096]{1,0:T(8,128)(2,1)S(1)}, bf16[8,4096]{1,0:T(8,128)(2,1)S(1)}, u32[]{:S(2)}, u32[]{:S(2)}) collective-permute-start(bf16[8,4096]{1,0:T(8,128)(2,1)S(1)} %get-tuple-element.35), channel_id=1, source_target_pairs={{0,1},{1,0},{2,3},{3,2},{4,5},{5,4},{6,7},{7,6},{8,9},{9,8},{10,11... | collective-permute-start | bytes 196616 | tf_op jit(solution)/shard_map/ppermute | solution.py:420
  76.4 1.8 %collective-permute-done.16.refs_3_ = bf16[8,4096]{1,0:T(8,128)(2,1)S(1)} collective-permute-done((bf16[8,4096]{1,0:T(8,128)(2,1)S(1)}, bf16[8,4096]{1,0:T(8,128)(2,1)S(1)}, u32[]{:S(2)}, u32[]{:S(2)}) %collective-permute-start.16) | collective-permute-done | bytes 65568 | tf_op jit(solution)/shard_map/ppermute | solution.py:420
  78.2 2.4 %collective-permute-done.15.refs_2_ = bf16[8,4096]{1,0:T(8,128)(2,1)S(1)} collective-permute-done((bf16[8,4096]{1,0:T(8,128)(2,1)S(1)}, bf16[8,4096]{1,0:T(8,128)(2,1)S(1)}, u32[]{:S(2)}, u32[]{:S(2)}) %collective-permute-start.15) | collective-permute-done | bytes 65568 | tf_op jit(solution)/shard_map/ppermute | solution.py:420
  80.6 1.1 %mix_back.1 = bf16[8,4096]{1,0:T(8,128)(2,1)} custom-call(f32[8,128]{1,0:T(8,128)S(1)} %get-tuple-element.18.info_ref.refs_8_, bf16[8,4096]{1,0:T(8,128)(2,1)S(1)} %get-tuple-element.36.refs_0_, bf16[8,4096]{1,0:T(8,128)(2,1)S(1)} %collective-permute-done.14.refs_1_, bf16[8,4096]{1,0:T(8,128)(2,1)S(1)} %collective-permute-done.15.refs_2_, ...), custom_call_target="tpu_custom_call" | custom-call | tf_op jit(solution)/shard_map/mix_back/pallas_call | solution.py:128
  (15 shorter events, 0.1 us)
Async XLA Ops:
  1.8 11.2 %collective-permute-start.2 = (bf16[8,4224]{1,0:T(8,128)(2,1)S(1)}, bf16[8,4224]{1,0:T(8,128)(2,1)S(1)}, u32[]{:S(2)}, u32[]{:S(2)}) collective-permute-start(bf16[8,4224]{1,0:T(8,128)(2,1)S(1)} %get-tuple-element.19.after_ref.refs_0_), channel_id=1, source_target_pairs={{0,3},{1,2},{2,1},{3,0},{4,7},{5,6},{6,5},{7,4},{8,11},{9,10},{10,... | collective-permute-start | bytes 202760 | tf_op jit(solution)/shard_map/ppermute | solution.py:387
  7.0 6.1 %collective-permute-start.1 = (bf16[8,4224]{1,0:T(8,128)(2,1)S(1)}, bf16[8,4224]{1,0:T(8,128)(2,1)S(1)}, u32[]{:S(2)}, u32[]{:S(2)}) collective-permute-start(bf16[8,4224]{1,0:T(8,128)(2,1)S(1)} %get-tuple-element.19.after_ref.refs_0_), channel_id=1, source_target_pairs={{0,2},{1,3},{2,0},{3,1},{4,6},{5,7},{6,4},{7,5},{8,10},{9,11},{10,... | collective-permute-start | bytes 202760 | tf_op jit(solution)/shard_map/ppermute | solution.py:387
  7.0 6.1 %collective-permute-start = (bf16[8,4224]{1,0:T(8,128)(2,1)S(1)}, bf16[8,4224]{1,0:T(8,128)(2,1)S(1)}, u32[]{:S(2)}, u32[]{:S(2)}) collective-permute-start(bf16[8,4224]{1,0:T(8,128)(2,1)S(1)} %get-tuple-element.19.after_ref.refs_0_), channel_id=1, source_target_pairs={{0,1},{1,0},{2,3},{3,2},{4,5},{5,4},{6,7},{7,6},{8,9},{9,8},{10,11... | collective-permute-start | bytes 202760 | tf_op jit(solution)/shard_map/ppermute | solution.py:387
  13.1 8.7 %collective-permute-start.4 = (bf16[32,4224]{1,0:T(8,128)(2,1)S(1)}, bf16[32,4224]{1,0:T(8,128)(2,1)S(1)}, u32[]{:S(2)}, u32[]{:S(2)}) collective-permute-start(bf16[32,4224]{1,0:T(8,128)(2,1)S(1)} %shard_map.74.after_ref.refs_0_), channel_id=1, source_target_pairs={{0,16},{4,20},{8,24},{12,28},{16,0},{20,4},{24,8},{28,12},{1,17},{... | collective-permute-start | bytes 811016 | tf_op jit(solution)/shard_map/ppermute | solution.py:394
  14.8 7.3 %collective-permute-start.3 = (bf16[32,4224]{1,0:T(8,128)(2,1)S(1)}, bf16[32,4224]{1,0:T(8,128)(2,1)S(1)}, u32[]{:S(2)}, u32[]{:S(2)}) collective-permute-start(bf16[32,4224]{1,0:T(8,128)(2,1)S(1)} %shard_map.74.after_ref.refs_0_), channel_id=1, source_target_pairs={{0,8},{4,12},{8,0},{12,4},{16,24},{20,28},{24,16},{28,20},{1,9},{5... | collective-permute-start | bytes 811016 | tf_op jit(solution)/shard_map/ppermute | solution.py:393
  22.3 6.5 %collective-permute-start.5 = (bf16[32,4224]{1,0:T(8,128)(2,1)S(1)}, bf16[32,4224]{1,0:T(8,128)(2,1)S(1)}, u32[]{:S(2)}, u32[]{:S(2)}) collective-permute-start(bf16[32,4224]{1,0:T(8,128)(2,1)S(1)} %shard_map.76.after_ref), channel_id=1, source_target_pairs={{0,8},{4,20},{8,0},{12,28},{16,24},{20,4},{24,16},{28,12},{1,9},{5... | collective-permute-start | bytes 811016 | tf_op jit(solution)/shard_map/ppermute | solution.py:398
  23.8 7.8 %collective-permute-start.6 = (bf16[32,4224]{1,0:T(8,128)(2,1)S(1)}, bf16[32,4224]{1,0:T(8,128)(2,1)S(1)}, u32[]{:S(2)}, u32[]{:S(2)}) collective-permute-start(bf16[32,4224]{1,0:T(8,128)(2,1)S(1)} %shard_map.74.after_ref.refs_0_), channel_id=1, source_target_pairs={{0,4},{4,0},{8,12},{12,8},{16,20},{20,16},{24,28},{28,24},{1,5},{5... | collective-permute-start | bytes 811016 | tf_op jit(solution)/shard_map/ppermute | solution.py:395
  23.8 7.8 %collective-permute-start.8 = (bf16[32,4224]{1,0:T(8,128)(2,1)S(1)}, bf16[32,4224]{1,0:T(8,128)(2,1)S(1)}, u32[]{:S(2)}, u32[]{:S(2)}) collective-permute-start(bf16[32,4224]{1,0:T(8,128)(2,1)S(1)} %collective-permute-done.4.first_ref.refs_2_), channel_id=1, source_target_pairs={{0,4},{4,0},{8,12},{12,8},{16,20},{20,16},{24,28},{28,24},{1,5},{5... | collective-permute-start | bytes 811016 | tf_op jit(solution)/shard_map/ppermute | solution.py:400
  24.3 7.3 %collective-permute-start.7 = (bf16[32,4224]{1,0:T(8,128)(2,1)S(1)}, bf16[32,4224]{1,0:T(8,128)(2,1)S(1)}, u32[]{:S(2)}, u32[]{:S(2)}) collective-permute-start(bf16[32,4224]{1,0:T(8,128)(2,1)S(1)} %collective-permute-done.3.second_ref.refs_1_), channel_id=1, source_target_pairs={{0,4},{4,0},{8,12},{12,8},{16,20},{20,16},{24,28},{28,24},{1,5},{5... | collective-permute-start | bytes 811016 | tf_op jit(solution)/shard_map/ppermute | solution.py:399
  28.8 2.9 %collective-permute-start.9 = (bf16[32,4224]{1,0:T(8,128)(2,1)S(1)}, bf16[32,4224]{1,0:T(8,128)(2,1)S(1)}, u32[]{:S(2)}, u32[]{:S(2)}) collective-permute-start(bf16[32,4224]{1,0:T(8,128)(2,1)S(1)} %collective-permute-done.5.refs_3_), channel_id=1, source_target_pairs={{0,4},{4,0},{8,12},{12,8},{16,20},{20,16},{24,28},{28,24},{1,5},{5... | collective-permute-start | bytes 811016 | tf_op jit(solution)/shard_map/ppermute | solution.py:402
  52.4 2.9 %collective-permute-start.10 = (bf16[128,4096]{1,0:T(8,128)(2,1)S(1)}, bf16[128,4096]{1,0:T(8,128)(2,1)S(1)}, u32[]{:S(2)}, u32[]{:S(2)}) collective-permute-start(bf16[128,4096]{1,0:T(8,128)(2,1)S(1)} %get-tuple-element.30), channel_id=1, source_target_pairs={{0,4},{4,0},{8,12},{12,8},{16,20},{20,16},{24,28},{28,24},{1,5},{5... | collective-permute-start | bytes 3145736 | tf_op jit(solution)/shard_map/ppermute | solution.py:408
  56.0 6.6 %collective-permute-start.11 = (bf16[32,4096]{1,0:T(8,128)(2,1)}, bf16[32,4096]{1,0:T(8,128)(2,1)S(1)}, u32[]{:S(2)}, u32[]{:S(2)}) collective-permute-start(bf16[32,4096]{1,0:T(8,128)(2,1)} %add_convert_fusion.1), channel_id=1, source_target_pairs={{0,8},{4,20},{8,0},{12,28},{16,24},{20,4},{24,16},{28,12},{1,9},{5... | collective-permute-start | bytes 786440 | tf_op jit(solution)/shard_map/ppermute | solution.py:412
  62.8 7.8 %collective-permute-start.12 = (bf16[32,4096]{1,0:T(8,128)(2,1)S(1)}, bf16[32,4096]{1,0:T(8,128)(2,1)S(1)}, u32[]{:S(2)}, u32[]{:S(2)}) collective-permute-start(bf16[32,4096]{1,0:T(8,128)(2,1)S(1)} %get-tuple-element.31), channel_id=1, source_target_pairs={{0,8},{4,12},{8,0},{12,4},{16,24},{20,28},{24,16},{28,20},{1,9},{5... | collective-permute-start | bytes 786440 | tf_op jit(solution)/shard_map/ppermute | solution.py:415
  64.4 7.5 %collective-permute-start.13 = (bf16[32,4096]{1,0:T(8,128)(2,1)S(1)}, bf16[32,4096]{1,0:T(8,128)(2,1)S(1)}, u32[]{:S(2)}, u32[]{:S(2)}) collective-permute-start(bf16[32,4096]{1,0:T(8,128)(2,1)S(1)} %get-tuple-element.32), channel_id=1, source_target_pairs={{0,16},{4,20},{8,24},{12,28},{16,0},{20,4},{24,8},{28,12},{1,17},{... | collective-permute-start | bytes 786440 | tf_op jit(solution)/shard_map/ppermute | solution.py:416
  72.0 6.2 %collective-permute-start.16 = (bf16[8,4096]{1,0:T(8,128)(2,1)S(1)}, bf16[8,4096]{1,0:T(8,128)(2,1)S(1)}, u32[]{:S(2)}, u32[]{:S(2)}) collective-permute-start(bf16[8,4096]{1,0:T(8,128)(2,1)S(1)} %get-tuple-element.33), channel_id=1, source_target_pairs={{0,3},{1,2},{2,1},{3,0},{4,7},{5,6},{6,5},{7,4},{8,11},{9,10},{10,... | collective-permute-start | bytes 196616 | tf_op jit(solution)/shard_map/ppermute | solution.py:420
  75.4 5.2 %collective-permute-start.15 = (bf16[8,4096]{1,0:T(8,128)(2,1)S(1)}, bf16[8,4096]{1,0:T(8,128)(2,1)S(1)}, u32[]{:S(2)}, u32[]{:S(2)}) collective-permute-start(bf16[8,4096]{1,0:T(8,128)(2,1)S(1)} %get-tuple-element.34), channel_id=1, source_target_pairs={{0,2},{1,3},{2,0},{3,1},{4,6},{5,7},{6,4},{7,5},{8,10},{9,11},{10,... | collective-permute-start | bytes 196616 | tf_op jit(solution)/shard_map/ppermute | solution.py:420
  75.4 5.2 %collective-permute-start.14 = (bf16[8,4096]{1,0:T(8,128)(2,1)S(1)}, bf16[8,4096]{1,0:T(8,128)(2,1)S(1)}, u32[]{:S(2)}, u32[]{:S(2)}) collective-permute-start(bf16[8,4096]{1,0:T(8,128)(2,1)S(1)} %get-tuple-element.35), channel_id=1, source_target_pairs={{0,1},{1,0},{2,3},{3,2},{4,5},{5,4},{6,7},{7,6},{8,9},{9,8},{10,11... | collective-permute-start | bytes 196616 | tf_op jit(solution)/shard_map/ppermute | solution.py:420
